TPU v7x, 256 devices: a whole 4x4x8 slice. The times are simulated.
256 devices in a mesh: rows: 64 (over y, z, x_hi), mem: 4 (over x_lo, core).
Axes of the slice: x: 4 (x_hi: 2, x_lo: 2; x = x_hi * 2 + x_lo), y: 4, z: 8, core: 2. Of those that a mesh axis runs over, the one named last changes fastest.
Arguments:
- state: float32 [16384, 5120], P('rows', 'mem')
- member_level: int32 [5120], P('mem'), may hold values from 0 to 3, as said below
- level_weight: float32 [4], replicated, may hold values from 0.3 to 3
- obs_row: int32 [1024], replicated, may hold values from 0 to 16383
- state_coords: int32 [2, 16384], replicated, may hold values from 0 to 255, as said below
- weights: float32 [1024, 5120], P('rows', 'mem'), may hold values from -6 to 6
Outputs:
- increment: float32 [16384, 5120], P('rows', 'mem')
Inputs may be any that keep to these rules, and one draw needn't show every extreme that they name: `member_level`: every one of the 4 levels holds at least 2 members. `state_coords`: the first coordinate of row i lies within 2 of i // 64.
All inputs are finite; a program needn't handle non-finite values.
Results may differ from a plain program's by a relative error of at most 0.000073.
Values sent between devices are 32-bit elements; how exact they have to be, the bound alone decides.
A program may use at most 64 MiB of HBM per device.

v0:
```python
import jax
import jax.numpy as jnp
from jax import lax
from jax.sharding import Mesh
from jax.sharding import PartitionSpec as P

LEVELS = 4
XCOL_DEV = 4
ROWS = ("rows_0", "rows_1", "rows_2")


def from_everyone(array, axis):
    copies = jnp.broadcast_to(array, (lax.axis_size(axis), *array.shape))
    return lax.all_to_all(copies, axis, split_axis=0, concat_axis=0, tiled=True)


def over_copies(array, axis):
    return from_everyone(array, axis).sum(axis=0)


def together(arrays, axis):
    line, at, gathered = (jnp.concatenate([a.reshape(-1) for a in arrays]), 0, [])
    total = over_copies(line, axis)
    for a in arrays:
        gathered.append(total[at : at + a.size].reshape(a.shape))
        at += a.size
    return tuple(gathered)


def own_rows(total, axes):
    for axis in axes:
        total = lax.psum_scatter(total, axis, scatter_dimension=0, tiled=True)
    return total


def over_pieces(array, axis):
    return lax.all_gather(array, axis).sum(0)


def taper_rows(state_coords, obs_row, row_first, row_total, radius):
    state_xy = lax.dynamic_slice_in_dim(state_coords, row_first, row_total, 1)
    observed_xy = jnp.take(state_coords, obs_row, axis=1)
    offset_x = state_xy[0][:, None] - observed_xy[0][None, :]
    offset_y = state_xy[1][:, None] - observed_xy[1][None, :]
    distance = offset_x * offset_x + offset_y * offset_y
    reach = jnp.maximum(0.0, 1.0 - distance.astype(jnp.float32) / float(radius * radius))
    return reach * reach


def on_device(state, member_level, level_weight, obs_row, state_coords, weights):
    highest = lax.Precision.HIGHEST
    radius = XCOL_DEV * lax.axis_size(ROWS)
    row_count = state.shape[0]
    row_first = lax.axis_index(ROWS) * row_count
    onehot = (member_level[:, None] == jnp.arange(LEVELS, dtype=jnp.int32)[None, :]).astype(
        jnp.float32
    )
    part_sums = jnp.dot(state, onehot, precision=highest, preferred_element_type=jnp.float32)
    part_counts = jnp.sum(onehot, axis=0)
    sums, counts = together((part_sums, part_counts), "mem")
    means = sums / counts[None, :]
    anomaly = state - jnp.take(means, member_level, axis=1)
    level_scale = level_weight / (counts - 1.0)
    scaled = anomaly * jnp.take(level_scale, member_level)[None, :]
    wanted = obs_row - row_first
    inside = (wanted >= 0) & (wanted < row_count)
    picked = jnp.take(anomaly, jnp.clip(wanted, 0, row_count - 1), axis=0)
    observed_mine = own_rows(jnp.where(inside[:, None], picked, 0.0), ROWS)
    observed = lax.all_gather(observed_mine, ROWS, axis=0, tiled=True)
    cross = jnp.dot(scaled, observed.T, precision=highest, preferred_element_type=jnp.float32)
    summed = over_pieces(cross, "mem")
    tapered = summed * taper_rows(state_coords, obs_row, row_first, row_count, radius)
    all_weights = lax.all_gather(weights, ROWS, axis=0, tiled=True)
    return jnp.dot(tapered, all_weights, precision=highest, preferred_element_type=jnp.float32)


def solution(mesh):
    split = Mesh(
        mesh.devices.reshape(4, 8, 2, mesh.shape["mem"]), ("rows_0", "rows_1", "rows_2", "mem")
    )
    return jax.shard_map(
        on_device,
        mesh=split,
        in_specs=(P(ROWS, "mem"), P("mem"), P(), P(), P(), P(ROWS, "mem")),
        out_specs=P(ROWS, "mem"),
        check_vma=False,
    )
```

profile of v0, /device:TPU:1, one launch (start us, length us, event | category | flops | bytes accessed | tf_op | source)
XLA Modules:
  0.0 499.1 jit_solution(5203281602962534624)
XLA Ops:
  6.5 0.9 convert_reduce_fusion
  7.5 2.0 convolution_bitcast_fusion
  9.5 0.2 copy.20
  9.7 0.1 reshape.43
  9.8 0.6 broadcast_in_dim.63
  10.4 6.4 %all-to-all-start = ((f32[4,1,1028]{2,1,0:T(1,128)}), f32[4,1,1028]{2,1,0:T(1,128)S(1)}, u32[]{:S(2)}, u32[]{:S(2)}) async-start(f32[4,1,1028]{2,1,0:T(1,128)} %broadcast_in_dim.63), calls=%async_computation | async-start | bytes 36864 | tf_op jit(solution)/shard_map/all_to_all | solution.py:14
  16.9 0.0 reduce-scatter.4.cloned.1.call-start
  16.9 0.0 copy-done.1
  16.9 0.0 copy-done.3
  17.0 0.0 copy-start.4
  17.0 1.5 copy.23
  18.4 1.6 all-to-all-done
  20.1 0.1 reshape.44
  20.2 0.1 copy.22
  20.3 0.1 broadcast_divide_fusion
  20.3 3.2 gather_fusion
  23.5 1.6 bitcast_subtract_fusion
  25.1 0.4 copy.24
  25.5 5.8 %gather_fusion.1 = f32[1024,1280]{1,0:T(8,128)} fusion(f32[256,1280]{1,0:T(8,128)S(1)} %copy.24, s32[1024]{0:T(1024)S(1)} %get-tuple-element.15), kind=kCustom, calls=%fused_computation.1 | custom fusion | bytes 10489856 | tf_op jit(solution)/shard_map/jit(_take)/gather | solution.py:67
  31.3 4.6 select_select_fusion
  35.8 0.0 reduce-scatter.4.cloned.1.call-update
  35.8 0.0 reduce-scatter.6.cloned.1.call-start
  35.9 59.4 %reduce-scatter.4.cloned.1.call-done = f32[256,1280]{1,0:T(8,128)} async-done(((f32[1024,1280]{1,0:T(8,128)}), f32[256,1280]{1,0:T(8,128)}) %reduce-scatter.4.cloned.1.call-update) | async-done | bytes 1310736 | tf_op jit(solution)/shard_map/reduce_scatter | solution.py:32
  95.3 0.0 reduce-scatter.6.cloned.1.call-update
  95.3 0.0 reduce-scatter.8.cloned.1.call-start
  95.3 37.8 %reduce-scatter.6.cloned.1.call-done = f32[32,1280]{1,0:T(8,128)} async-done(((f32[256,1280]{1,0:T(8,128)}), f32[32,1280]{1,0:T(8,128)}) %reduce-scatter.6.cloned.1.call-update) | async-done | bytes 163856 | tf_op jit(solution)/shard_map/reduce_scatter | solution.py:32
  133.2 0.0 reduce-scatter.8.cloned.1.call-update
  133.2 0.0 all-gather.5.cloned.1.call-start
  133.2 22.5 %reduce-scatter.8.cloned.1.call-done = f32[16,1280]{1,0:T(8,128)} async-done(((f32[32,1280]{1,0:T(8,128)}), f32[16,1280]{1,0:T(8,128)}) %reduce-scatter.8.cloned.1.call-update) | async-done | bytes 81936 | tf_op jit(solution)/shard_map/reduce_scatter | solution.py:32
  155.7 0.0 all-gather.5.cloned.1.call-update
  155.7 0.2 all-gather.9.cloned.1.call-start
  156.0 0.6 fusion.28
  156.6 2.5 select_select_fusion.1
  159.1 0.0 copy-start.2
  159.2 129.3 %all-gather.5.cloned.1.call-done = f32[1024,1280]{1,0:T(8,128)} async-done(((f32[16,1280]{1,0:T(8,128)}), f32[1024,1280]{1,0:T(8,128)}) %all-gather.5.cloned.1.call-update) | async-done | bytes 5242896 | tf_op jit(solution)/shard_map/all_gather | solution.py:69
  288.5 12.1 %fusion = f32[256,1024]{1,0:T(8,128)} fusion(f32[1024,1280]{1,0:T(8,128)} %all-gather.5.cloned.1.call-done, f32[256,1280]{0,1:T(8,128)S(1)} %bitcast_subtract_fusion, f32[1280]{0:T(1024)S(1)} %select_select_fusion.1), kind=kOutput, calls=%fused_computation.5 | convolution fusion | flops 4026859520 | bytes 7607296 | tf_op jit(solution)/shard_map/dot_general | solution.py:70
  300.6 0.0 all-gather.9.cloned.1.call-update
  300.6 0.3 all-gather.7.cloned.1.call-start
  300.9 0.3 all-gather.7.cloned.1.call-update
  301.2 5.0 copy.25
  306.2 6.2 %gather_fusion.2 = s32[1024,2]{1,0:T(8,128)S(1)} fusion(s32[2,16384]{0,1:T(8,128)} %copy.25, s32[1024]{0:T(1024)S(1)} %get-tuple-element.14), kind=kCustom, calls=%fused_computation.2 | custom fusion | bytes 20480 | tf_op jit(solution)/shard_map/jit(_take)/gather | solution.py:42
  312.4 0.1 constant_dynamic-slice_fusion
  312.5 0.2 select_bitcast_fusion
  312.7 0.5 slice_reduce_fusion.1
  313.2 37.0 %all-gather.9.cloned.1.call-done = f32[1024,1024]{1,0:T(8,128)} async-done(((f32[256,1024]{1,0:T(8,128)}), f32[1024,1024]{1,0:T(8,128)}) %all-gather.9.cloned.1.call-update) | async-done | bytes 4194320 | tf_op jit(solution)/shard_map/all_gather | solution.py:37
  350.2 2.7 reduce_sum.29
  352.9 130.9 %all-gather.7.cloned.1.call-done = f32[1024,1280]{1,0:T(8,128)} async-done(((f32[16,1280]{1,0:T(8,128)}), f32[1024,1280]{1,0:T(8,128)}) %all-gather.7.cloned.1.call-update) | async-done | bytes 5242896 | tf_op jit(solution)/shard_map/all_gather | solution.py:73
  483.8 8.4 %fusion.2 = f32[256,1280]{1,0:T(8,128)} fusion(f32[1024,1280]{1,0:T(8,128)} %all-gather.7.cloned.1.call-done, f32[256,1024]{1,0:T(8,128)S(1)} %reduce_sum.29, s32[1024]{0:T(1024)S(1)} %get-tuple-element.6, s32[256]{0:T(256)S(1)} %bitcast.18, s32[1024]{0:T(1024)S(1)} %get-tuple-element.5, s32[256]{0:T(256)S(1)} %bitcast.17), kind=kOutput, calls=%fused_computation.8 | convolution fusion | flops 4029415424 | bytes 7612416 | tf_op jit(solution)/shard_map/dot_general | solution.py:74
  (15 shorter events, 0.1 us)
Async XLA Ops:
  6.5 10.3 %copy-start.1 = (s32[1280]{0:T(1024)S(1)}, s32[1280]{0:T(1024)}, u32[]{:S(2)}) copy-start(s32[1280]{0:T(1024)} %param.7) | copy-start | bytes 15364
  6.5 10.4 %copy-start = (f32[256,1280]{1,0:T(8,128)S(1)}, f32[256,1280]{1,0:T(8,128)}, u32[]{:S(2)}) copy-start(f32[256,1280]{1,0:T(8,128)} %param.6) | copy-start | bytes 3932164
  6.5 10.4 %copy-start.3 = (s32[1024]{0:T(1024)S(1)}, s32[1024]{0:T(1024)}, u32[]{:S(2)}) copy-start(s32[1024]{0:T(1024)} %param.9) | copy-start | bytes 12292
  10.4 9.6 %all-to-all-start = ((f32[4,1,1028]{2,1,0:T(1,128)}), f32[4,1,1028]{2,1,0:T(1,128)S(1)}, u32[]{:S(2)}, u32[]{:S(2)}) async-start(f32[4,1,1028]{2,1,0:T(1,128)} %broadcast_in_dim.63), calls=%async_computation | async-start | bytes 36864 | tf_op jit(solution)/shard_map/all_to_all | solution.py:14
  16.9 78.4 %reduce-scatter.4.cloned.1.call-start = ((), (), s32[]{:S(2)}) async-start(), calls=%async_computation.4 | async-start | bytes 6553600 | tf_op jit(solution)/shard_map/reduce_scatter | solution.py:32
  17.0 3.1 copy-start.4
  35.8 97.3 %reduce-scatter.6.cloned.1.call-start = ((), (), s32[]{:S(2)}) async-start(), calls=%async_computation.5 | async-start | bytes 1474560 | tf_op jit(solution)/shard_map/reduce_scatter | solution.py:32
  95.3 60.4 %reduce-scatter.8.cloned.1.call-start = ((), (), s32[]{:S(2)}) async-start(), calls=%async_computation.6 | async-start | bytes 245760 | tf_op jit(solution)/shard_map/reduce_scatter | solution.py:32
  133.2 155.3 %all-gather.5.cloned.1.call-start = ((), (), s32[]{:S(2)}) async-start(), calls=%async_computation.7 | async-start | bytes 5324800 | tf_op jit(solution)/shard_map/all_gather | solution.py:69
  155.7 194.5 %all-gather.9.cloned.1.call-start = ((), (), s32[]{:S(2)}) async-start(), calls=%async_computation.9 | async-start | bytes 5242880 | tf_op jit(solution)/shard_map/all_gather | solution.py:37
  159.1 142.1 %copy-start.2 = (s32[2,16384]{1,0:T(2,128)S(1)}, s32[2,16384]{1,0:T(2,128)}, u32[]{:S(2)}) copy-start(s32[2,16384]{1,0:T(2,128)} %param.10) | copy-start | bytes 393220
  300.6 183.2 %all-gather.7.cloned.1.call-start = ((), (), s32[]{:S(2)}) async-start(), calls=%async_computation.8 | async-start | bytes 5324800 | tf_op jit(solution)/shard_map/all_gather | solution.py:73
Sparse Core Ops, SparseCore 0:
  36.0 59.2 reduce-scatter.3
  97.8 35.3 reduce-scatter.5
  135.6 20.0 reduce-scatter.7
  159.2 129.2 all-gather.4
  300.8 49.3 all-gather.8
  353.7 130.0 all-gather.6
where the time goes:
time: 502 us; the launch traced here: 499 us
  waiting for transfers between devices  419 us (83%)
  local copies, waits for them, and re-layouts  24.3 us (5%)
  matrix products  22.6 us (5%)
  between operations  13.7 us (3%)
  other arithmetic  12.7 us (3%)
  starting transfers between devices  7.02 us (1%)
    all_gather x1, waiting for transfers between devices, on_device(): all_weights = lax.all_gather(weights, ROWS, axis=0, tiled=True)  131 us
    all_gather x1, waiting for transfers between devices, on_device(): observed = lax.all_gather(observed_mine, ROWS, axis=0, tiled=True)  129 us
    reduce_scatter x3, waiting for transfers between devices, own_rows(): total = lax.psum_scatter(total, axis, scatter_dimension=0, tiled=True)  120 us
    all_gather x1, waiting for transfers between devices, over_pieces(): return lax.all_gather(array, axis).sum(0)  37 us
    dot_general x1, matrix products, on_device(): jnp.dot(scaled, observed.T, precision=highest, preferred_element_type=jnp...  12.1 us
  transfers between devices with their start and end apart: 7, of which 7 were waited for; matrix products, arithmetic and copies ran while one was open for 4% of the time, Pallas kernels for 0%

commit v1 on v0

v1 whole, which is shorter than its diff:
```python
import functools

import jax
import jax.numpy as jnp
from jax import lax
from jax.experimental import pallas as pl
from jax.experimental.pallas import tpu as pltpu
from jax.sharding import PartitionSpec as P

MESH = pl.DeviceIdType.MESH
LEVELS = 4
NX, NY, NZ = 4, 4, 8
RADIUS = 256
F32 = jnp.float32
BF16 = jnp.bfloat16
NT = (((1,), (1,)), ((), ()))
NN = (((1,), (0,)), ((), ()))
COPIES = 192


def split(value):
    high = value.astype(BF16)
    return high, (value - high.astype(F32)).astype(BF16)


def dot(a, b, dims=NN):
    return lax.dot_general(a, b, dims, preferred_element_type=F32)


def dot3(a, b, dims=NN):
    return dot(a[0], b[0], dims) + dot(a[0], b[1], dims) + dot(a[1], b[0], dims)


def turns(chains):
    chains = list(chains)
    while chains:
        left = []
        for chain in chains:
            try:
                next(chain)
                left.append(chain)
            except StopIteration:
                pass
        chains = left
        if chains:
            yield


def in_turn(*parts):
    for part in parts:
        yield from part()


def drain(chain):
    for _ in chain:
        pass


def advance(chain, count):
    for _ in range(count):
        next(chain, None)


def kernel(
    state, level_all, level_kept, level_weight, obs_col, obs_row, table, row_xy, w_in,
    out,
    sums, kept, relay, s_high, s_low, pick_a, pick_b, got_az, got_ay, got_by, got_bz,
    seen_a, seen_b, w_a, w_b, cross, cross_in, got_x, t_all, send_sem, recv_sem,
):
    rows, mem = lax.axis_index("rows"), lax.axis_index("mem")
    y, z, xh = rows // (NZ * 2), (rows // 2) % NZ, rows % 2
    xl, core = mem // 2, mem % 2
    x = xh * 2 + xl
    count = [0]
    sent = []

    def at_y(k):
        return ((k * NZ + z) * 2 + xh, mem)

    def at_z(k):
        return ((y * NZ + k) * 2 + xh, mem)

    def at_x(k, c):
        return ((y * NZ + z) * 2 + k // 2, (k % 2) * 2 + c)

    def put(src, dst, device, landing=None):
        number = count[0]
        count[0] += 1
        out_copy = pltpu.make_async_remote_copy(
            src_ref=src, dst_ref=dst, send_sem=send_sem.at[number], recv_sem=recv_sem.at[number],
            device_id=device, device_id_type=MESH)
        out_copy.start()
        sent.append(out_copy)
        landing = dst if landing is None else landing
        return pltpu.make_async_remote_copy(
            src_ref=landing, dst_ref=landing, send_sem=send_sem.at[number],
            recv_sem=recv_sem.at[number], device_id=device, device_id_type=MESH)

    def gather_ring(n, p, block, device):
        def chain(way, half):
            hops = n // 2 if (half == 0) == (way == 1) else n // 2 - 1
            arriving = None
            for s in range(1, hops + 1):
                if arriving is not None:
                    arriving.wait_recv()
                out_block = block((p - way * (s - 1) + n) % n, half)
                in_block = block((p - way * s + n) % n, half)
                arriving = put(out_block, out_block, device((p + way + n) % n), in_block)
                yield
            if arriving is not None:
                arriving.wait_recv()
        return turns([chain(1, 0), chain(-1, 1), chain(1, 1), chain(-1, 0)])

    def scatter_ring(n, p, block, landing, device):
        def chain(way, half):
            hops = n // 2 if (half == 0) == (way == 1) else n // 2 - 1
            direction = 0 if way == 1 else 1
            arriving = None
            for s in range(1, hops + 1):
                part = block((p + way * (hops - s + 1) + n) % n, half)
                if arriving is not None:
                    arriving.wait_recv()
                    part[...] += landing[direction, half, s - 2]
                arriving = put(part, landing.at[direction, half, s - 1], device((p + way + n) % n))
                yield
            if arriving is not None:
                arriving.wait_recv()
                block(p, half)[...] += landing[direction, half, hops - 1]
        return turns([chain(1, 0), chain(-1, 1), chain(1, 1), chain(-1, 0)])

    def gather_plane(buf_a, buf_b):
        nb = buf_a.shape[2] // 2
        first = in_turn(
            lambda: gather_ring(NY, y, lambda k, h: buf_a.at[k, z, pl.ds(h * nb, nb)], at_y),
            lambda: gather_ring(NZ, z, lambda k, h: buf_a.at[pl.ds(h * (NY // 2), NY // 2), k], at_z))
        second = in_turn(
            lambda: gather_ring(NZ, z, lambda k, h: buf_b.at[y, k, pl.ds(h * nb, nb)], at_z),
            lambda: gather_ring(NY, y, lambda k, h: buf_b.at[k, pl.ds(h * (NZ // 2), NZ // 2)], at_y))
        return turns([second, first])

    def scatter_plane(buf_a, buf_b):
        nb = buf_a.shape[2] // 2
        first = in_turn(
            lambda: scatter_ring(NZ, z, lambda k, h: buf_a.at[pl.ds(h * (NY // 2), NY // 2), k], got_az, at_z),
            lambda: scatter_ring(NY, y, lambda k, h: buf_a.at[k, z, pl.ds(h * nb, nb)], got_ay, at_y))
        second = in_turn(
            lambda: scatter_ring(NY, y, lambda k, h: buf_b.at[k, pl.ds(h * (NZ // 2), NZ // 2)], got_by, at_y),
            lambda: scatter_ring(NZ, z, lambda k, h: buf_b.at[y, k, pl.ds(h * nb, nb)], got_bz, at_z))
        return turns([second, first])

    friends = [at_y((y + 1) % NY), at_y((y + NY - 1) % NY), at_z((z + 1) % NZ), at_z((z + NZ - 1) % NZ)]
    line = [at_x((x + d) % NX, c) for d in range(1, NX) for c in (core, 1 - core)]
    line.append(at_x(x, 1 - core))
    barrier = pltpu.get_barrier_semaphore()
    for device in friends + line:
        pl.semaphore_signal(barrier, inc=1, device_id=device, device_id_type=MESH)

    block_rows, members = state.shape
    half_members = members // 2
    level_ids = lax.broadcasted_iota(jnp.int32, (8, members), 0)
    own_level = level_all[...]
    onehot = (level_ids == own_level).astype(F32)
    counted = jnp.sum((level_ids - LEVELS == own_level).astype(F32), axis=1, keepdims=True)
    part = lax.dot_general(onehot, state[...], NT, precision=lax.Precision.HIGHEST, preferred_element_type=F32)
    sums[x * 2 + core] = part + counted

    depth, width_a = w_in.shape[0], w_a.shape[3]
    w_a[y, z, pl.ds(xh * depth, depth)] = w_in[:, :width_a]
    w_b[y, z, pl.ds(xh * depth, depth)] = w_in[:, width_a:]
    mine = pl.ds(pl.multiple_of(xh * half_members, 128), half_members)
    theirs = pl.ds(pl.multiple_of((1 - xh) * half_members, 128), half_members)
    kept[xh] = state[:, mine]

    pl.semaphore_wait(barrier, len(friends) + len(line))

    sums_in = []
    for d in range(1, NX):
        for c in (0, 1):
            device = at_x((x + d) % NX, (core + c) % 2)
            from_x, from_core = (x - d + NX) % NX, (core + c) % 2
            sums_in.append(put(sums.at[x * 2 + core], sums.at[x * 2 + core], device, sums.at[from_x * 2 + from_core]))
    sums_in.append(put(sums.at[x * 2 + core], sums.at[x * 2 + core], at_x(x, 1 - core), sums.at[x * 2 + 1 - core]))
    partner = at_x((x + 2) % NX, core)
    own_part, other_part = pl.ds(xh * depth, depth), pl.ds((1 - xh) * depth, depth)
    w_pair = [put(buf.at[y, z, own_part], buf.at[y, z, own_part], partner, buf.at[y, z, other_part]) for buf in (w_b, w_a)]
    piece = block_rows // 4
    first_hop = []
    for k in (0, 2, 1, 3):
        way = 1 if k < 2 else NX - 1
        first_hop.append((k, way, put(state.at[pl.ds(k * piece, piece), theirs], relay.at[k], at_x((x + way) % NX, core))))

    def relay_on(number):
        k, way, arriving = first_hop[number]
        arriving.wait_recv()
        origin = ((x - way + NX) % NX) // 2
        spot = pl.ds(k * piece, piece)
        return put(relay.at[k], kept.at[origin, spot], at_x((x + way) % NX, core), kept.at[1 - xh, spot])

    for arriving in w_pair:
        arriving.wait_recv()
    w_chain = gather_plane(w_a, w_b)
    advance(w_chain, 1)

    for arriving in sums_in:
        arriving.wait_recv()
    kept_level = level_kept[...]
    total = [sums[h * 4] + sums[h * 4 + 1] + sums[h * 4 + 2] + sums[h * 4 + 3] for h in (0, 1)]
    means = [(t / jnp.concatenate([t[LEVELS:], t[LEVELS:]], axis=0)).T for t in total]
    scale = jnp.zeros((1, half_members), F32)
    for l in range(LEVELS):
        value = level_weight[l] / (total[0][LEVELS + l : LEVELS + l + 1, 0:1] - 1.0)
        scale = jnp.where(kept_level == l, value, scale)
    block = rows // 2

    def prepare(h, first):
        mean = jnp.where(h == 0, means[0], means[1])
        shift = jnp.zeros((block_rows, half_members), F32)
        for l in range(LEVELS):
            shift = jnp.where(kept_level == l, mean[:, l : l + 1], shift)
        anomaly = kept[h] - shift
        high, low = split(anomaly * scale)
        s_high[h], s_low[h] = high, low
        high, low = split(anomaly)
        row_ids = lax.broadcasted_iota(jnp.int32, (NY * 64, block_rows), 1) + (block * 2 + h) * block_rows
        per = NY * 64
        for k in range(obs_col.shape[0] // per):
            chosen = (obs_col[pl.ds(k * per, per)] == row_ids).astype(BF16)
            picked = dot(chosen, high) + dot(chosen, low)
            a = picked[:, : pick_a.shape[3]].reshape(NZ, per // NZ, pick_a.shape[3])
            b = picked[:, pick_a.shape[3] :].reshape(NZ, per // NZ, pick_b.shape[3])
            pick_a[k] = a if first else pick_a[k] + a
            pick_b[k] = b if first else pick_b[k] + b

    final_hop = [relay_on(0), relay_on(1)]
    advance(w_chain, 1)
    prepare(xh, True)
    final_hop += [relay_on(2), relay_on(3)]
    advance(w_chain, 2)
    for arriving in final_hop:
        arriving.wait_recv()
    prepare(1 - xh, False)
    advance(w_chain, 1)

    drain(scatter_plane(pick_a, pick_b))
    advance(w_chain, 1)
    seen_a[y, z] = pick_a[y, z]
    seen_b[y, z] = pick_b[y, z]
    drain(gather_plane(seen_a, seen_b))
    advance(w_chain, 1)

    wide_a = seen_a.shape[3]
    s_a = [jnp.concatenate([ref[0, :, :wide_a], ref[1, :, :wide_a]], axis=0) for ref in (s_high, s_low)]
    s_b = [jnp.concatenate([ref[0, :, wide_a:], ref[1, :, wide_a:]], axis=0) for ref in (s_high, s_low)]
    per = NZ * seen_a.shape[2]
    for k in range(NY):
        o_a = split(seen_a[k].reshape(per, wide_a))
        o_b = split(seen_b[k].reshape(per, seen_b.shape[3]))
        c = dot3(s_a, o_a, NT) + dot3(s_b, o_b, NT)
        cross[:, :, :, k * per : (k + 1) * per] = c.reshape(NX, 2, c.shape[0] // (2 * NX), per).swapaxes(0, 1)

    pair = put(cross.at[1 - core], cross_in, at_x(x, 1 - core))
    pair.wait_recv()
    cross[core] += cross_in[...]
    rows_each = cross.shape[2]
    advance(w_chain, 1)
    drain(scatter_ring(NX, x, lambda k, h: cross.at[core, k, pl.ds(h * (rows_each // 2), rows_each // 2)], got_x,
                       lambda k: at_x(k, core)))
    advance(w_chain, 1)

    seen_rows = obs_row[...]
    high_ids = lax.broadcasted_iota(jnp.int32, (128, seen_rows.shape[1]), 0)
    is_high = (high_ids == seen_rows // 128).astype(BF16)
    is_low = high_ids == seen_rows % 128
    seen_x = jnp.sum(jnp.where(is_low, dot(table[0], is_high), 0.0), axis=0, keepdims=True)
    seen_y = jnp.sum(jnp.where(is_low, dot(table[1], is_high), 0.0), axis=0, keepdims=True)
    apart_x = row_xy[:, 0:1] - seen_x
    apart_y = row_xy[:, 1:2] - seen_y
    reach = jnp.maximum(0.0, 1.0 - (apart_x * apart_x + apart_y * apart_y) / float(RADIUS * RADIUS))
    t_all[mem] = cross[core, x] * (reach * reach)

    across = put(t_all.at[mem], t_all.at[mem], at_x(xh * 2 + 1 - xl, core), t_all.at[(1 - xl) * 2 + core])
    beside = put(t_all.at[mem], t_all.at[mem], at_x(x, 1 - core), t_all.at[xl * 2 + 1 - core])
    advance(w_chain, 1)
    across.wait_recv()
    there = (1 - xl) * 2
    passed = put(t_all.at[there + core], t_all.at[there + core], at_x(x, 1 - core), t_all.at[there + 1 - core])
    drain(w_chain)
    beside.wait_recv()
    passed.wait_recv()

    t = split(t_all[...].reshape(block_rows, t_all.shape[2]))
    step = 256
    for buf, start in ((w_a, 0), (w_b, width_a)):
        for k in range(buf.shape[3] // step):
            w = split(buf[:, :, :, k * step : (k + 1) * step].reshape(t_all.shape[2], step))
            out[:, start + k * step : start + (k + 1) * step] = dot3(t, w)

    for copy in sent:
        copy.wait_send()


def on_device(state, member_level, level_weight, obs_row, state_coords, weights):
    rows, mem = lax.axis_index("rows"), lax.axis_index("mem")
    block_rows, members = state.shape
    observations = obs_row.shape[0]
    half = members // 2
    kept = lax.dynamic_slice_in_dim(member_level, (rows % 2) * half, half)
    own = block_rows // 4
    row_xy = lax.dynamic_slice_in_dim(state_coords, rows * block_rows + mem * own, own, 1).T.astype(F32)
    table = state_coords.reshape(2, -1, 128).swapaxes(1, 2).astype(BF16)
    depth = weights.shape[0]
    per = 2 * depth
    a, b = half * 2 // 5, half * 3 // 5
    hy, hz = NY // 2, NZ // 2
    vmem = pl.BlockSpec(memory_space=pltpu.VMEM)
    smem = pl.BlockSpec(memory_space=pltpu.SMEM)
    return pl.pallas_call(
        kernel,
        out_shape=jax.ShapeDtypeStruct((block_rows, members), F32),
        in_specs=[vmem, vmem, vmem, smem, vmem, vmem, vmem, vmem, vmem],
        out_specs=vmem,
        scratch_shapes=[
            pltpu.VMEM((NX * 2, 8, block_rows), F32),
            pltpu.VMEM((2, block_rows, half), F32),
            pltpu.VMEM((4, block_rows // 4, half), F32),
            pltpu.VMEM((2, block_rows, half), BF16),
            pltpu.VMEM((2, block_rows, half), BF16),
            pltpu.VMEM((NY, NZ, per, a), F32),
            pltpu.VMEM((NY, NZ, per, b), F32),
            pltpu.VMEM((2, 2, hz, hy, per, a), F32),
            pltpu.VMEM((2, 2, hy, per // 2, a), F32),
            pltpu.VMEM((2, 2, hy, hz, per, b), F32),
            pltpu.VMEM((2, 2, hz, per // 2, b), F32),
            pltpu.VMEM((NY, NZ, per, a), F32),
            pltpu.VMEM((NY, NZ, per, b), F32),
            pltpu.VMEM((NY, NZ, per, members * 2 // 5), F32),
            pltpu.VMEM((NY, NZ, per, members * 3 // 5), F32),
            pltpu.VMEM((2, NX, own, observations), F32),
            pltpu.VMEM((NX, own, observations), F32),
            pltpu.VMEM((2, 2, 2, own // 2, observations), F32),
            pltpu.VMEM((4, own, observations), F32),
            pltpu.SemaphoreType.DMA((COPIES,)),
            pltpu.SemaphoreType.DMA((COPIES,)),
        ],
        compiler_params=pltpu.CompilerParams(
            collective_id=0, has_side_effects=True, vmem_limit_bytes=60 * 1024 * 1024),
    )(
        state, member_level.reshape(1, -1), kept.reshape(1, -1), level_weight,
        obs_row.reshape(-1, 1), obs_row.reshape(1, -1), table, row_xy, weights,
    )


def solution(mesh):
    return jax.shard_map(
        on_device,
        mesh=mesh,
        in_specs=(P("rows", "mem"), P("mem"), P(), P(), P(), P("rows", "mem")),
        out_specs=P("rows", "mem"),
        check_vma=False,
    )
```

time: 502 us -> 147 us (0.29)
  waiting for transfers between devices: 419 us -> 0 us
  Pallas kernels: 0 us -> 137 us
  matrix products: 22.6 us -> 0 us
  local copies, waits for them, and re-layouts: 24.3 us -> 8.4 us
  between operations: 13.7 us -> 0.02 us
  other arithmetic: 12.7 us -> 1.56 us
  starting transfers between devices: 7.02 us -> 0 us
    all_gather x3 -> x0, waiting for transfers between devices: 297 us -> none  [the longest x1 131 us: on_device(): all_weights = lax.all_gather(weights, ROWS, axis=0, tiled=True)]
    pallas_call x0 -> x1, Pallas kernels: none -> 137 us  [on_device(): pl.pallas_call(kernel, out_shape=jax.ShapeDtypeStruct((block_rows, member...]
    reduce_scatter x3 -> x0, waiting for transfers between devices: 120 us -> none  [own_rows(): total = lax.psum_scatter(total, axis, scatter_dimension=0, tiled=True)]
    dot_general x3 -> x0, matrix products: 22.6 us -> none  [the longest x1 12.1 us: on_device(): jnp.dot(scaled, observed.T, precision=highest, preferred_element_type=jnp...]
    gather x4 -> x0, local copies, waits for them, and re-layouts: 15.7 us -> none  [the longest x1 6.18 us: taper_rows(): observed_xy = jnp.take(state_coords, obs_row, axis=1)]
    select_n x4 -> x0, other arithmetic: 7.32 us -> none  [the longest x1 4.56 us: on_device(): observed_mine = own_rows(jnp.where(inside[:, None], picked, 0.0), ROWS)]
    all_to_all x1 -> x0, starting transfers between devices: 6.42 us -> none  [from_everyone(): return lax.all_to_all(copies, axis, split_axis=0, concat_axis=0, tiled=True)]
  transfers between devices with their start and end apart: 7 -> 0, of which waited for: 7 -> 0; matrix products, arithmetic and copies ran while one was open for 4% -> 0% of each run, Pallas kernels for 0% -> 0%
where the time goes in v1:
time: 147 us
  Pallas kernels  137 us (93%)
  local copies, waits for them, and re-layouts  8.4 us (6%)
  other arithmetic  1.56 us (1%)
    pallas_call x1, Pallas kernels, on_device(): pl.pallas_call(kernel, out_shape=jax.ShapeDtypeStruct((block_rows, member...  137 us

profile of v1, /device:TPU:1, one launch (start us, length us, event | category | flops | bytes accessed | tf_op | source)
XLA Modules:
  0.0 146.6 jit_solution(10395394585583136843)
XLA Ops:
  0.0 0.7 constant_dynamic-slice_fusion
  0.8 0.8 dynamic_slice.6
  1.5 0.6 reshape.15.level_kept
  2.1 1.3 reshape.14.level_all
  3.4 0.1 copy.11
  3.5 0.6 convert_bitcast_fusion.1.row_xy
  4.1 0.9 convert_bitcast_fusion
  5.1 0.7 copy.8
  5.8 1.7 %copy.10.obs_col = s32[1024,1]{1,0:T(8,128)} copy(s32[1024,1]{0,1:T(1,128)} %bitcast.12) | data formatting | bytes 8192 | tf_op jit(solution)/shard_map/reshape | solution.py:349
  7.5 136.6 %shard_map.64 = f32[256,1280]{1,0:T(8,128)} custom-call(f32[256,1280]{1,0:T(8,128)} %state.1, s32[1,1280]{1,0:T(1,128)} %reshape.14.level_all, s32[1,640]{1,0:T(1,128)} %reshape.15.level_kept, f32[4]{0:T(128)} %level_weight.1, s32[1024,1]{1,0:T(8,128)} %copy.10.obs_col, s32[1,1024]{1,0:T(1,128)} %bitcast.13, bf16[2,128,128]{2,1,0:T(8,128)(2,1)} %bitcast.10, ...), custom_call_target="tpu_custom_call" | custom-call | tf_op jit(solution)/shard_map/pallas_call | solution.py:317
  144.1 2.5 %copy.16 = f32[256,1280]{1,0:T(8,128)} copy(f32[256,1280]{1,0:T(8,128)} %shard_map.64) | data formatting | bytes 2621440
  (1 shorter events, 0.0 us)

commit v2 on v1

v2 whole, which is shorter than its diff:
```python
import math

import jax
import jax.numpy as jnp
from jax import lax
from jax.experimental import pallas as pl
from jax.experimental.pallas import tpu as pltpu
from jax.sharding import PartitionSpec as P

MESH = pl.DeviceIdType.MESH
LEVELS = 4
NX, NY, NZ = 4, 4, 8
RADIUS = 256
F32 = jnp.float32
BF16 = jnp.bfloat16
NT = (((1,), (1,)), ((), ()))
NN = (((1,), (0,)), ((), ()))
COPIES = 229
PIECES = 8
VMEM_BYTES = 67043328
SENDS = 16
STRAIGHT = 4


def split(value):
    high = value.astype(BF16)
    return high, (value - high.astype(F32)).astype(BF16)


def dot(a, b, dims=NN):
    return lax.dot_general(a, b, dims, preferred_element_type=F32)


def dot3(a, b, dims=NN):
    return dot(a[0], b[0], dims) + dot(a[0], b[1], dims) + dot(a[1], b[0], dims)


def turns(chains):
    chains = list(chains)
    while chains:
        left = []
        for chain in chains:
            try:
                next(chain)
                left.append(chain)
            except StopIteration:
                pass
        chains = left
        if chains:
            yield


def drain(chain):
    for _ in chain:
        pass


def advance(chain, count):
    for _ in range(count):
        next(chain, None)


def kernel(
    state_far, level_far, level_weight, obs_far, coords_far, w_far,
    out,
    state, level_line, obs_line, coords, w_in, table,
    sums, kept, relay, s_high, s_low, pick_a, pick_b, got_az, got_ay, got_by, got_bz,
    seen_a, seen_b, w_a, w_b, cross, cross_in, got_x, t_all, ledger, send_sem, recv_sem, straight_sem, load_sem,
):
    rows, mem = lax.axis_index("rows"), lax.axis_index("mem")
    y, z, xh = rows // (NZ * 2), (rows // 2) % NZ, rows % 2
    xl, core = mem // 2, mem % 2
    x = xh * 2 + xl
    count = [0]
    sent = []

    def at_y(k):
        return ((k * NZ + z) * 2 + xh, mem)

    def at_z(k):
        return ((y * NZ + k) * 2 + xh, mem)

    def at_x(k, c):
        return ((y * NZ + z) * 2 + k // 2, (k % 2) * 2 + c)

    def put(src, dst, device, landing=None, arrival=None):
        recv = recv_sem.at[count[0]]
        if arrival is None:
            arrival = recv
            count[0] += 1
        group = len(sent) % SENDS
        copy = pltpu.make_async_remote_copy(
            src_ref=src, dst_ref=dst, send_sem=send_sem.at[group], recv_sem=arrival,
            device_id=device, device_id_type=MESH)
        copy.start()
        sent.append(math.prod(src.shape) // 128)
        if arrival is not recv:
            return None
        landing = dst if landing is None else landing
        return pltpu.make_async_remote_copy(
            src_ref=landing, dst_ref=landing, send_sem=send_sem.at[group],
            recv_sem=arrival, device_id=device, device_id_type=MESH)

    def all_lines(lines, semaphore):
        whole = ledger.at[pl.ds(0, lines)]
        return pltpu.make_async_remote_copy(
            src_ref=whole, dst_ref=whole, send_sem=semaphore, recv_sem=semaphore,
            device_id=at_x(x, 1 - core), device_id_type=MESH)

    def gather_ring(n, p, block, device, only=None):
        def chain(way, half):
            hops = n // 2 if (half == 0) == (way == 1) else n // 2 - 1
            arriving = None
            for s in range(1, hops + 1):
                if arriving is not None:
                    arriving.wait_recv()
                out_block = block((p - way * (s - 1) + n) % n, half)
                in_block = block((p - way * s + n) % n, half)
                arriving = put(out_block, out_block, device((p + way + n) % n), in_block)
                yield
            if arriving is not None:
                arriving.wait_recv()
        order = [(1, 0), (-1, 1), (1, 1), (-1, 0)]
        return turns([chain(way, half) for way, half in order if only in (None, half)])

    def scatter_ring(n, p, block, landing, device):
        def chain(way, half):
            hops = n // 2 if (half == 0) == (way == 1) else n // 2 - 1
            direction = 0 if way == 1 else 1
            arriving = None
            for s in range(1, hops + 1):
                part = block((p + way * (hops - s + 1) + n) % n, half)
                if arriving is not None:
                    arriving.wait_recv()
                    part[...] += landing[direction, half, s - 2]
                arriving = put(part, landing.at[direction, half, s - 1], device((p + way + n) % n))
                yield
            if arriving is not None:
                arriving.wait_recv()
                block(p, half)[...] += landing[direction, half, hops - 1]
        return turns([chain(1, 0), chain(-1, 1), chain(1, 1), chain(-1, 0)])

    def far_first(n):
        return sorted(range(1, n), key=lambda d: abs(d - n // 2))

    def scatter_straight(n, p, block, landing, device, arrival):
        for d in far_first(n):
            q = (p + d) % n
            put(block(q), landing.at[d - 1], device(q), arrival=arrival)
        yield
        all_lines((n - 1) * math.prod(landing.shape[1:]) // 128, arrival).wait_recv()
        block(p)[...] += sum(landing[d - 1] for d in range(1, n))

    def gather_straight(n, p, block, device, arrival):
        for d in far_first(n):
            put(block(p), block(p), device((p + d) % n), arrival=arrival)
        yield
        all_lines((n - 1) * math.prod(block(p).shape) // 128, arrival).wait_recv()

    def gather_fine(n, p, outer, inner):
        going, done, r = [inner(p)], False, 0
        while going or not done:
            if not done:
                try:
                    next(outer)
                except StopIteration:
                    done = True
                if r > 0:
                    going.append(inner((p + r) % n))
                    if 2 * r < n:
                        going.append(inner((p - r + n) % n))
                r += 1
            left = []
            for chain in going:
                try:
                    next(chain)
                    left.append(chain)
                except StopIteration:
                    pass
            going = left
            yield

    def part(h):
        return pl.ds((h + xh) % 2 * w_in.shape[0], w_in.shape[0])

    def y_outer(buf, own):
        return gather_fine(
            NY, y, gather_ring(NY, y, lambda k, h: buf.at[k, z, part(h)], at_y, own),
            lambda j: gather_ring(NZ, z, lambda k, h: buf.at[j, k, part(h)], at_z, own))

    def z_outer(buf, own):
        return gather_fine(
            NZ, z, gather_ring(NZ, z, lambda k, h: buf.at[y, k, part(h)], at_z, own),
            lambda j: gather_ring(NY, y, lambda k, h: buf.at[k, j, part(h)], at_y, own))

    friends = [at_y((y + 1) % NY), at_y((y + NY - 1) % NY), at_z((z + 1) % NZ), at_z((z + NZ - 1) % NZ)]
    line = [at_x((x + d) % NX, c) for d in range(1, NX) for c in (core, 1 - core)]
    line.append(at_x(x, 1 - core))
    barrier = pltpu.get_barrier_semaphore()
    for device in friends + line:
        pl.semaphore_signal(barrier, inc=1, device_id=device, device_id_type=MESH)

    loads = [pltpu.make_async_copy(far, near, load_sem.at[n]) for n, (far, near) in enumerate((
        (w_far, w_in), (state_far, state), (level_far, level_line), (obs_far, obs_line), (coords_far, coords)))]
    for load in loads:
        load.start()
    block_rows, members = state.shape
    half_members = members // 2
    observations = obs_line.shape[0]
    loads[0].wait()
    depth, width_a = w_in.shape[0], w_a.shape[3]
    w_a[y, z, pl.ds(xh * depth, depth)] = w_in[:, :width_a]
    w_b[y, z, pl.ds(xh * depth, depth)] = w_in[:, width_a:]
    mine = pl.ds(pl.multiple_of(xh * half_members, 128), half_members)
    theirs = pl.ds(pl.multiple_of((1 - xh) * half_members, 128), half_members)

    for load in loads[1:]:
        load.wait()
    level_all = level_line[...].reshape(1, members)
    obs_all = obs_line[...].reshape(1, observations)
    pl.semaphore_wait(barrier, len(friends) + len(line))

    partner = at_x((x + 2) % NX, core)
    own_part, other_part = pl.ds(xh * depth, depth), pl.ds((1 - xh) * depth, depth)
    w_pair = [put(buf.at[y, z, own_part], buf.at[y, z, own_part], partner, buf.at[y, z, other_part]) for buf in (w_b, w_a)]
    piece = block_rows // PIECES
    hops = []
    for n in range(PIECES):
        k = n // 2 + (n % 2) * (PIECES // 2)
        way = 1 if n % 2 == 0 else NX - 1
        hops.append((k, way, put(state.at[pl.ds(k * piece, piece), theirs], relay.at[k], at_x((x + way) % NX, core))))

    def pass_on(numbers):
        landed = []
        for n in numbers:
            k, way, arriving = hops[n]
            arriving.wait_recv()
            origin = ((x - way + NX) % NX) // 2
            spot = pl.ds(k * piece, piece)
            landed.append(put(relay.at[k], kept.at[origin, spot], at_x((x + way) % NX, core), kept.at[1 - xh, spot]))
        return landed

    level_ids = lax.broadcasted_iota(jnp.int32, (8, members), 0)
    own_level = level_all
    onehot = (level_ids == own_level).astype(F32)
    counted = jnp.sum((level_ids - LEVELS == own_level).astype(F32), axis=1, keepdims=True)
    summed = lax.dot_general(onehot, state[...], NT, precision=lax.Precision.HIGHEST, preferred_element_type=F32)
    sums[x * 2 + core] = summed + counted
    sums_in = []
    for d in range(1, NX):
        for c in (0, 1):
            device = at_x((x + d) % NX, (core + c) % 2)
            from_x, from_core = (x - d + NX) % NX, (core + c) % 2
            sums_in.append(put(sums.at[x * 2 + core], sums.at[x * 2 + core], device, sums.at[from_x * 2 + from_core]))
    sums_in.append(put(sums.at[x * 2 + core], sums.at[x * 2 + core], at_x(x, 1 - core), sums.at[x * 2 + 1 - core]))
    kept[xh] = state[:, mine]
    kept_level = jnp.where(xh == 0, level_all[:, :half_members], level_all[:, half_members:])
    block = rows // 2
    obs_col = jnp.broadcast_to(obs_all, (8, observations)).T[:, 0:1]

    def move_weights():
        own = turns([z_outer(w_b, 0), y_outer(w_a, 0)])
        other = turns([z_outer(w_b, 1), y_outer(w_a, 1)])
        next(own)
        for arriving in w_pair:
            arriving.wait_recv()
        next(other)
        yield
        yield from turns([own, other])

    for k in range(table.shape[1]):
        table[:, k, :] = coords[:, k * 128 : (k + 1) * 128]

    w_chain = move_weights()
    advance(w_chain, 1)
    landed = pass_on(range(0, PIECES // 2))
    advance(w_chain, 1)
    landed += pass_on(range(PIECES // 2, PIECES))
    for arriving in sums_in:
        arriving.wait_recv()
    total = [sums[h * 4] + sums[h * 4 + 1] + sums[h * 4 + 2] + sums[h * 4 + 3] for h in (0, 1)]
    means = [(t / jnp.concatenate([t[LEVELS:], t[LEVELS:]], axis=0)).T for t in total]
    scale = jnp.zeros((1, half_members), F32)
    for l in range(LEVELS):
        value = level_weight[l] / (total[0][LEVELS + l : LEVELS + l + 1, 0:1] - 1.0)
        scale = jnp.where(kept_level == l, value, scale)

    wide_a = pick_a.shape[3]
    per = NZ * pick_a.shape[2]

    def prepare(h, first):
        mean = jnp.where(h == 0, means[0], means[1])
        shift = jnp.zeros((block_rows, half_members), F32)
        for l in range(LEVELS):
            shift = jnp.where(kept_level == l, mean[:, l : l + 1], shift)
        anomaly = kept[h] - shift
        s_high[h], s_low[h] = split(anomaly * scale)
        high, low = split(anomaly)
        row_ids = lax.broadcasted_iota(jnp.int32, (per, block_rows), 1) + (block * 2 + h) * block_rows
        for k in range(NY):
            chosen = (obs_col[k * per : (k + 1) * per] == row_ids).astype(BF16)
            picked = dot(chosen, high) + dot(chosen, low)
            a = picked[:, :wide_a].reshape(NZ, per // NZ, wide_a)
            b = picked[:, wide_a:].reshape(NZ, per // NZ, half_members - wide_a)
            pick_a[k] = a if first else pick_a[k] + a
            pick_b[k] = b if first else pick_b[k] + b

    prepare(xh, True)
    advance(w_chain, 1)
    for arriving in landed:
        arriving.wait_recv()
    prepare(1 - xh, False)

    nb = pick_a.shape[2] // 2
    hy, hz = NY // 2, NZ // 2
    a_chain = scatter_ring(NZ, z, lambda k, h: pick_a.at[pl.ds(h * hy, hy), k], got_az, at_z)
    b_chain = scatter_ring(NY, y, lambda k, h: pick_b.at[k, pl.ds(h * hz, hz)], got_by, at_y)
    advance(b_chain, 1)
    advance(a_chain, 1)
    advance(a_chain, 1)
    advance(b_chain, 1)
    advance(a_chain, 1)
    drain(b_chain)
    b_near = scatter_straight(NZ, z, lambda k: pick_b.at[y, k], got_bz, at_z, straight_sem.at[0])
    advance(b_near, 1)
    drain(a_chain)
    a_near = scatter_straight(NY, y, lambda k: pick_a.at[k, z], got_ay, at_y, straight_sem.at[1])
    advance(a_near, 1)
    drain(b_near)
    seen_b[y, z] = pick_b[y, z]
    b_near = gather_straight(NZ, z, lambda k: seen_b.at[y, k], at_z, straight_sem.at[2])
    advance(b_near, 1)
    drain(a_near)
    seen_a[y, z] = pick_a[y, z]
    a_near = gather_straight(NY, y, lambda k: seen_a.at[k, z], at_y, straight_sem.at[3])
    advance(a_near, 1)
    advance(w_chain, 1)
    drain(a_near)
    a_chain = gather_ring(NZ, z, lambda k, h: seen_a.at[pl.ds(h * hy, hy), k], at_z)
    advance(a_chain, 1)
    drain(b_near)
    b_chain = gather_ring(NY, y, lambda k, h: seen_b.at[k, pl.ds(h * hz, hz)], at_y)
    advance(b_chain, 1)
    advance(a_chain, 1)
    advance(a_chain, 1)
    advance(b_chain, 1)
    advance(a_chain, 1)
    drain(b_chain)
    drain(a_chain)

    seen_rows = obs_all
    high_ids = lax.broadcasted_iota(jnp.int32, (128, observations), 0)
    is_high = (high_ids == seen_rows // 128).astype(BF16)
    is_low = high_ids == seen_rows % 128
    seen_at = [jnp.sum(jnp.where(is_low, dot(table[i].astype(F32).T.astype(BF16), is_high), 0.0), axis=0, keepdims=True)
               for i in (0, 1)]
    row_start = pl.multiple_of(rows * block_rows + xl * 128, 128)
    near = coords[:, pl.ds(row_start, 128)].astype(F32)
    near = jnp.concatenate([near] * 4, axis=0).T
    own = near.shape[0] // 2
    row_at = jnp.where(core == 0, near[:own], near[own:])


    def covariance(k):
        o = [seen[k].reshape(per, seen.shape[3]) for seen in (seen_a, seen_b)]
        c = dot3([ref[...].reshape(2 * block_rows, half_members) for ref in (s_high, s_low)],
                 split(jnp.concatenate(o, axis=1)), NT)
        cross[k] = c.reshape(NX, 2, own, per).swapaxes(0, 1)
        pair = put(cross.at[k, 1 - core], cross_in.at[k], at_x(x, 1 - core))
        yield
        pair.wait_recv()
        cross[k, core] += cross_in[k]
        yield from scatter_ring(
            NX, x, lambda i, h: cross.at[k, core, i, pl.ds(h * (own // 2), own // 2)], got_x.at[k],
            lambda i: at_x(i, core))
        cols = slice(k * per, (k + 1) * per)
        apart_x = row_at[:, 0:1] - seen_at[0][:, cols]
        apart_y = row_at[:, 1:2] - seen_at[1][:, cols]
        reach = jnp.maximum(0.0, 1.0 - (apart_x * apart_x + apart_y * apart_y) / float(RADIUS * RADIUS))
        t_all[k, mem] = cross[k, core, x] * (reach * reach)
        across = put(t_all.at[k, mem], t_all.at[k, mem], at_x(xh * 2 + 1 - xl, core), t_all.at[k, (1 - xl) * 2 + core])
        beside = put(t_all.at[k, mem], t_all.at[k, mem], at_x(x, 1 - core), t_all.at[k, xl * 2 + 1 - core])
        yield
        across.wait_recv()
        there = (1 - xl) * 2
        passed = put(t_all.at[k, there + core], t_all.at[k, there + core], at_x(x, 1 - core),
                     t_all.at[k, there + 1 - core])
        yield
        beside.wait_recv()
        passed.wait_recv()

    for _ in turns([covariance(k) for k in range(NY)]):
        advance(w_chain, 1)
    drain(w_chain)

    t = [split(t_all[k].reshape(block_rows, per)) for k in range(NY)]
    t = [jnp.concatenate([piece[i] for piece in t], axis=1) for i in (0, 1)]
    step = 256
    for buf, start in ((w_a, 0), (w_b, width_a)):
        for k in range(buf.shape[3] // step):
            w = split(buf[:, :, :, k * step : (k + 1) * step].reshape(observations, step))
            out[:, start + k * step : start + (k + 1) * step] = dot3(t, w)

    for group in range(SENDS):
        all_lines(sum(sent[group::SENDS]), send_sem.at[group]).wait_send()
    assert count[0] == COPIES, count[0]
    assert max(sum(sent[group::SENDS]) for group in range(SENDS)) <= ledger.shape[0]


def on_device(state, member_level, level_weight, obs_row, state_coords, weights):
    block_rows, members = state.shape
    observations = obs_row.shape[0]
    half = members // 2
    own = block_rows // 4
    per = 2 * weights.shape[0]
    a, b = half * 3 // 5, half * 2 // 5
    hy, hz = NY // 2, NZ // 2
    line = observations // NY
    vmem = pl.BlockSpec(memory_space=pltpu.VMEM)
    smem = pl.BlockSpec(memory_space=pltpu.SMEM)
    hbm = pl.BlockSpec(memory_space=pltpu.HBM)
    return pl.pallas_call(
        kernel,
        out_shape=jax.ShapeDtypeStruct((block_rows, members), F32),
        in_specs=[hbm, hbm, smem, hbm, hbm, hbm],
        out_specs=vmem,
        scratch_shapes=[
            pltpu.VMEM(state.shape, F32),
            pltpu.VMEM(member_level.shape, jnp.int32),
            pltpu.VMEM(obs_row.shape, jnp.int32),
            pltpu.VMEM(state_coords.shape, jnp.int32),
            pltpu.VMEM(weights.shape, F32),
            pltpu.VMEM((2, state_coords.shape[1] // 128, 128), jnp.int32),
            pltpu.VMEM((NX * 2, 8, block_rows), F32),
            pltpu.VMEM((2, block_rows, half), F32),
            pltpu.VMEM((PIECES, block_rows // PIECES, half), F32),
            pltpu.VMEM((2, block_rows, half), BF16),
            pltpu.VMEM((2, block_rows, half), BF16),
            pltpu.VMEM((NY, NZ, per, a), F32),
            pltpu.VMEM((NY, NZ, per, b), F32),
            pltpu.VMEM((2, 2, hz, hy, per, a), F32),
            pltpu.VMEM((NY - 1, per, a), F32),
            pltpu.VMEM((2, 2, hy, hz, per, b), F32),
            pltpu.VMEM((NZ - 1, per, b), F32),
            pltpu.VMEM((NY, NZ, per, a), F32),
            pltpu.VMEM((NY, NZ, per, b), F32),
            pltpu.VMEM((NY, NZ, per, members * 2 // 5), F32),
            pltpu.VMEM((NY, NZ, per, members * 3 // 5), F32),
            pltpu.VMEM((NY, 2, NX, own, line), F32),
            pltpu.VMEM((NY, NX, own, line), F32),
            pltpu.VMEM((NY, 2, 2, 2, own // 2, line), F32),
            pltpu.VMEM((NY, 4, own, line), F32),
            pltpu.VMEM((2816, 128), F32),
            pltpu.SemaphoreType.DMA((SENDS,)),
            pltpu.SemaphoreType.DMA((COPIES,)),
            pltpu.SemaphoreType.DMA((STRAIGHT,)),
            pltpu.SemaphoreType.DMA((5,)),
        ],
        compiler_params=pltpu.CompilerParams(
            collective_id=0, has_side_effects=True, vmem_limit_bytes=VMEM_BYTES),
    )(
        state, member_level, level_weight, obs_row, state_coords, weights,
    )


def solution(mesh):
    return jax.shard_map(
        on_device,
        mesh=mesh,
        in_specs=(P("rows", "mem"), P("mem"), P(), P(), P(), P("rows", "mem")),
        out_specs=P("rows", "mem"),
        check_vma=False,
    )
```

time: 147 us -> 115 us (0.78)
  Pallas kernels: 137 us -> 112 us
  local copies, waits for them, and re-layouts: 8.4 us -> 2.46 us
  other arithmetic: 1.56 us -> 0 us
    pallas_call x1, Pallas kernels: 137 us -> 112 us  [on_device(): pl.pallas_call(kernel, out_shape=jax.ShapeDtypeStruct((block_rows, member...]
    reshape x3 -> x0, local copies, waits for them, and re-layouts: 3.59 us -> none  [the longest x1 1.71 us: on_device(): obs_row.reshape(-1, 1)]
    dynamic_slice x2 -> x0, local copies, waits for them, and re-layouts: 1.52 us -> none  [the longest x1 0.77 us: on_device(): kept = lax.dynamic_slice_in_dim(member_level, rows % 2 * half, half)]
where the time goes in v2:
time: 115 us
  Pallas kernels  112 us (97%)
  local copies, waits for them, and re-layouts  2.46 us (2%)
    pallas_call x1, Pallas kernels, on_device(): pl.pallas_call(kernel, out_shape=jax.ShapeDtypeStruct((block_rows, member...  112 us
    unnamed x1, local copies, waits for them, and re-layouts  2.46 us

profile of v2, /device:TPU:1, one launch (start us, length us, event | category | flops | bytes accessed | tf_op | source)
XLA Modules:
  0.0 114.5 jit_solution(17773649115209334008)
XLA Ops:
  0.0 112.1 %shard_map.64 = f32[256,1280]{1,0:T(8,128)} custom-call(f32[256,1280]{1,0:T(8,128)} %state_far.1, s32[1280]{0:T(1024)} %level_far.1, f32[4]{0:T(128)} %level_weight.1, s32[1024]{0:T(1024)} %obs_far.1, s32[2,16384]{1,0:T(2,128)} %coords_far.1, f32[16,1280]{1,0:T(8,128)} %w_far.1), custom_call_target="tpu_custom_call" | custom-call | tf_op jit(solution)/shard_map/pallas_call | solution.py:422
  112.1 2.5 %copy.8 = f32[256,1280]{1,0:T(8,128)} copy(f32[256,1280]{1,0:T(8,128)} %shard_map.64) | data formatting | bytes 2621440

commit v3 on v2

--- a/solution.py
+++ b/solution.py
@@ -65,14 +65,14 @@
     out,
     state, level_line, obs_line, coords, w_in, table,
     sums, kept, relay, s_high, s_low, pick_a, pick_b, got_az, got_ay, got_by, got_bz,
-    seen_a, seen_b, w_a, w_b, cross, cross_in, got_x, t_all, ledger, send_sem, recv_sem, straight_sem, load_sem,
+    seen_a, seen_b, w_a, w_b, cross, cross_in, got_x, t_all, seen_at, total_out, ledger, send_sem, recv_sem, straight_sem, load_sem,
 ):
     rows, mem = lax.axis_index("rows"), lax.axis_index("mem")
     y, z, xh = rows // (NZ * 2), (rows // 2) % NZ, rows % 2
     xl, core = mem // 2, mem % 2
     x = xh * 2 + xl
     count = [0]
-    sent = []
+    sent, leaving = [], []
 
     def at_y(k):
         return ((k * NZ + z) * 2 + xh, mem)
@@ -107,7 +107,7 @@
             src_ref=whole, dst_ref=whole, send_sem=semaphore, recv_sem=semaphore,
             device_id=at_x(x, 1 - core), device_id_type=MESH)
 
-    def gather_ring(n, p, block, device, only=None):
+    def gather_ring(n, p, block, device, only=None, late=False):
         def chain(way, half):
             hops = n // 2 if (half == 0) == (way == 1) else n // 2 - 1
             arriving = None
@@ -117,6 +117,8 @@
                 out_block = block((p - way * (s - 1) + n) % n, half)
                 in_block = block((p - way * s + n) % n, half)
                 arriving = put(out_block, out_block, device((p + way + n) % n), in_block)
+                yield
+            if late and hops < n // 2:
                 yield
             if arriving is not None:
                 arriving.wait_recv()
@@ -134,6 +136,8 @@
                     arriving.wait_recv()
                     part[...] += landing[direction, half, s - 2]
                 arriving = put(part, landing.at[direction, half, s - 1], device((p + way + n) % n))
+                yield
+            if hops < n // 2:
                 yield
             if arriving is not None:
                 arriving.wait_recv()
@@ -240,6 +244,9 @@
             landed.append(put(relay.at[k], kept.at[origin, spot], at_x((x + way) % NX, core), kept.at[1 - xh, spot]))
         return landed
 
+    w_own = turns([z_outer(w_b, 0), y_outer(w_a, 0)])
+    w_other = turns([z_outer(w_b, 1), y_outer(w_a, 1)])
+    advance(w_own, 1)
     level_ids = lax.broadcasted_iota(jnp.int32, (8, members), 0)
     own_level = level_all
     onehot = (level_ids == own_level).astype(F32)
@@ -258,24 +265,16 @@
     block = rows // 2
     obs_col = jnp.broadcast_to(obs_all, (8, observations)).T[:, 0:1]
 
-    def move_weights():
-        own = turns([z_outer(w_b, 0), y_outer(w_a, 0)])
-        other = turns([z_outer(w_b, 1), y_outer(w_a, 1)])
-        next(own)
-        for arriving in w_pair:
-            arriving.wait_recv()
-        next(other)
-        yield
-        yield from turns([own, other])
-
+    advance(w_own, 1)
+    for arriving in w_pair:
+        arriving.wait_recv()
+    advance(w_other, 1)
+    landed = pass_on(range(0, PIECES // 2))
+    advance(w_other, 1)
+    landed += pass_on(range(PIECES // 2, PIECES))
+    advance(w_own, 1)
     for k in range(table.shape[1]):
         table[:, k, :] = coords[:, k * 128 : (k + 1) * 128]
-
-    w_chain = move_weights()
-    advance(w_chain, 1)
-    landed = pass_on(range(0, PIECES // 2))
-    advance(w_chain, 1)
-    landed += pass_on(range(PIECES // 2, PIECES))
     for arriving in sums_in:
         arriving.wait_recv()
     total = [sums[h * 4] + sums[h * 4 + 1] + sums[h * 4 + 2] + sums[h * 4 + 3] for h in (0, 1)]
@@ -306,7 +305,8 @@
             pick_b[k] = b if first else pick_b[k] + b
 
     prepare(xh, True)
-    advance(w_chain, 1)
+    advance(w_other, 1)
+    w_chain = turns([w_own, w_other])
     for arriving in landed:
         arriving.wait_recv()
     prepare(1 - xh, False)
@@ -319,6 +319,7 @@
     advance(a_chain, 1)
     advance(a_chain, 1)
     advance(b_chain, 1)
+    advance(a_chain, 1)
     advance(a_chain, 1)
     drain(b_chain)
     b_near = scatter_straight(NZ, z, lambda k: pick_b.at[y, k], got_bz, at_z, straight_sem.at[0])
@@ -326,43 +327,45 @@
     drain(a_chain)
     a_near = scatter_straight(NY, y, lambda k: pick_a.at[k, z], got_ay, at_y, straight_sem.at[1])
     advance(a_near, 1)
+    seen_rows = obs_all
+    high_ids = lax.broadcasted_iota(jnp.int32, (128, observations), 0)
+    is_high = (high_ids == seen_rows // 128).astype(BF16)
+    is_low = high_ids == seen_rows % 128
+    for i in (0, 1):
+        found = dot(table[i].astype(F32).T.astype(BF16), is_high)
+        found = jnp.sum(jnp.where(is_low, found, 0.0), axis=0, keepdims=True)
+        for k in range(NY):
+            seen_at[i, k] = found[:, k * per : (k + 1) * per]
+    row_start = pl.multiple_of(rows * block_rows + xl * 128, 128)
+    near = coords[:, pl.ds(row_start, 128)].astype(F32)
+    near = jnp.concatenate([near] * 4, axis=0).T
+    own = near.shape[0] // 2
+    row_at = jnp.where(core == 0, near[:own], near[own:])
+
+
+    drain(a_near)
+    seen_a[y, z] = pick_a[y, z]
+    a_near = gather_straight(NY, y, lambda k: seen_a.at[k, z], at_y, straight_sem.at[3])
+    advance(a_near, 1)
     drain(b_near)
     seen_b[y, z] = pick_b[y, z]
     b_near = gather_straight(NZ, z, lambda k: seen_b.at[y, k], at_z, straight_sem.at[2])
     advance(b_near, 1)
     drain(a_near)
-    seen_a[y, z] = pick_a[y, z]
-    a_near = gather_straight(NY, y, lambda k: seen_a.at[k, z], at_y, straight_sem.at[3])
-    advance(a_near, 1)
-    advance(w_chain, 1)
-    drain(a_near)
-    a_chain = gather_ring(NZ, z, lambda k, h: seen_a.at[pl.ds(h * hy, hy), k], at_z)
+    a_chain = gather_ring(NZ, z, lambda k, h: seen_a.at[pl.ds(h * hy, hy), k], at_z, late=True)
     advance(a_chain, 1)
     drain(b_near)
     b_chain = gather_ring(NY, y, lambda k, h: seen_b.at[k, pl.ds(h * hz, hz)], at_y)
     advance(b_chain, 1)
     advance(a_chain, 1)
     advance(a_chain, 1)
+    advance(a_chain, 1)
     advance(b_chain, 1)
-    advance(a_chain, 1)
-    drain(b_chain)
     drain(a_chain)
 
-    seen_rows = obs_all
-    high_ids = lax.broadcasted_iota(jnp.int32, (128, observations), 0)
-    is_high = (high_ids == seen_rows // 128).astype(BF16)
-    is_low = high_ids == seen_rows % 128
-    seen_at = [jnp.sum(jnp.where(is_low, dot(table[i].astype(F32).T.astype(BF16), is_high), 0.0), axis=0, keepdims=True)
-               for i in (0, 1)]
-    row_start = pl.multiple_of(rows * block_rows + xl * 128, 128)
-    near = coords[:, pl.ds(row_start, 128)].astype(F32)
-    near = jnp.concatenate([near] * 4, axis=0).T
-    own = near.shape[0] // 2
-    row_at = jnp.where(core == 0, near[:own], near[own:])
-
-
     def covariance(k):
-        o = [seen[k].reshape(per, seen.shape[3]) for seen in (seen_a, seen_b)]
+        there_y = (y + k) % NY
+        o = [seen[there_y].reshape(per, seen.shape[3]) for seen in (seen_a, seen_b)]
         c = dot3([ref[...].reshape(2 * block_rows, half_members) for ref in (s_high, s_low)],
                  split(jnp.concatenate(o, axis=1)), NT)
         cross[k] = c.reshape(NX, 2, own, per).swapaxes(0, 1)
@@ -373,9 +376,8 @@
         yield from scatter_ring(
             NX, x, lambda i, h: cross.at[k, core, i, pl.ds(h * (own // 2), own // 2)], got_x.at[k],
             lambda i: at_x(i, core))
-        cols = slice(k * per, (k + 1) * per)
-        apart_x = row_at[:, 0:1] - seen_at[0][:, cols]
-        apart_y = row_at[:, 1:2] - seen_at[1][:, cols]
+        apart_x = row_at[:, 0:1] - seen_at[0, there_y]
+        apart_y = row_at[:, 1:2] - seen_at[1, there_y]
         reach = jnp.maximum(0.0, 1.0 - (apart_x * apart_x + apart_y * apart_y) / float(RADIUS * RADIUS))
         t_all[k, mem] = cross[k, core, x] * (reach * reach)
         across = put(t_all.at[k, mem], t_all.at[k, mem], at_x(xh * 2 + 1 - xl, core), t_all.at[k, (1 - xl) * 2 + core])
@@ -388,19 +390,38 @@
         yield
         beside.wait_recv()
         passed.wait_recv()
-
-    for _ in turns([covariance(k) for k in range(NY)]):
+        drain(w_chain)
+        t = split(t_all[k].reshape(block_rows, per))
+        step = 256
+        for buf, start in ((w_a, 0), (w_b, width_a)):
+            for n in range(buf.shape[3] // step):
+                w = split(buf[there_y, :, :, n * step : (n + 1) * step].reshape(per, step))
+                cols = slice(start + n * step, start + (n + 1) * step)
+                if k == 0:
+                    total_out[:, cols] = dot3(t, w)
+                else:
+                    total_out[:, cols] += dot3(t, w)
+                if k == NY // 2:
+                    leaving.append(pltpu.make_async_copy(
+                        total_out.at[:, pl.ds(cols.start, step)], out.at[:, pl.ds(cols.start, step)],
+                        load_sem.at[len(leaving)]))
+                    leaving[-1].start()
+
+    chains = [covariance(k) for k in range(NY)]
+    near_first = [0, 1, 3, 2]
+    next(chains[0])
+    advance(w_chain, 1)
+    next(chains[1])
+    next(chains[3])
+    for k in near_first[:3]:
+        next(chains[k])
+    drain(b_chain)
+    next(chains[2])
+    advance(w_chain, 1)
+    for n, _ in enumerate(turns([chains[k] for k in near_first])):
         advance(w_chain, 1)
-    drain(w_chain)
-
-    t = [split(t_all[k].reshape(block_rows, per)) for k in range(NY)]
-    t = [jnp.concatenate([piece[i] for piece in t], axis=1) for i in (0, 1)]
-    step = 256
-    for buf, start in ((w_a, 0), (w_b, width_a)):
-        for k in range(buf.shape[3] // step):
-            w = split(buf[:, :, :, k * step : (k + 1) * step].reshape(observations, step))
-            out[:, start + k * step : start + (k + 1) * step] = dot3(t, w)
-
+    for copy in leaving:
+        copy.wait()
     for group in range(SENDS):
         all_lines(sum(sent[group::SENDS]), send_sem.at[group]).wait_send()
     assert count[0] == COPIES, count[0]
@@ -413,17 +434,16 @@
     half = members // 2
     own = block_rows // 4
     per = 2 * weights.shape[0]
-    a, b = half * 3 // 5, half * 2 // 5
+    a, b = half * 2 // 5, half * 3 // 5
     hy, hz = NY // 2, NZ // 2
     line = observations // NY
-    vmem = pl.BlockSpec(memory_space=pltpu.VMEM)
     smem = pl.BlockSpec(memory_space=pltpu.SMEM)
     hbm = pl.BlockSpec(memory_space=pltpu.HBM)
     return pl.pallas_call(
         kernel,
         out_shape=jax.ShapeDtypeStruct((block_rows, members), F32),
         in_specs=[hbm, hbm, smem, hbm, hbm, hbm],
-        out_specs=vmem,
+        out_specs=hbm,
         scratch_shapes=[
             pltpu.VMEM(state.shape, F32),
             pltpu.VMEM(member_level.shape, jnp.int32),
@@ -450,6 +470,8 @@
             pltpu.VMEM((NY, NX, own, line), F32),
             pltpu.VMEM((NY, 2, 2, 2, own // 2, line), F32),
             pltpu.VMEM((NY, 4, own, line), F32),
+            pltpu.VMEM((2, NY, 1, line), F32),
+            pltpu.VMEM(state.shape, F32),
             pltpu.VMEM((2816, 128), F32),
             pltpu.SemaphoreType.DMA((SENDS,)),
             pltpu.SemaphoreType.DMA((COPIES,)),

time: 115 us -> 109 us (0.948)
  Pallas kernels: 112 us -> 107 us
    pallas_call x1, Pallas kernels: 112 us -> 107 us  [on_device(): pl.pallas_call(kernel, out_shape=jax.ShapeDtypeStruct((block_rows, member...]
where the time goes in v3:
time: 109 us
  Pallas kernels  107 us (98%)
  local copies, waits for them, and re-layouts  2.46 us (2%)
    pallas_call x1, Pallas kernels, on_device(): pl.pallas_call(kernel, out_shape=jax.ShapeDtypeStruct((block_rows, member...  107 us
    unnamed x1, local copies, waits for them, and re-layouts  2.46 us

profile of v3, /device:TPU:1, one launch (start us, length us, event | category | flops | bytes accessed | tf_op | source)
XLA Modules:
  0.0 109.1 jit_solution(15113194248259374743)
XLA Ops:
  0.0 106.7 %shard_map.64 = f32[256,1280]{1,0:T(8,128)} custom-call(f32[256,1280]{1,0:T(8,128)} %state_far.1, s32[1280]{0:T(1024)} %level_far.1, f32[4]{0:T(128)} %level_weight.1, s32[1024]{0:T(1024)} %obs_far.1, s32[2,16384]{1,0:T(2,128)} %coords_far.1, f32[16,1280]{1,0:T(8,128)} %w_far.1), custom_call_target="tpu_custom_call" | custom-call | tf_op jit(solution)/shard_map/pallas_call | solution.py:442
  106.7 2.5 %copy.8 = f32[256,1280]{1,0:T(8,128)} copy(f32[256,1280]{1,0:T(8,128)} %shard_map.64) | data formatting | bytes 2621440

commit v4 on v3

--- a/solution.py
+++ b/solution.py
@@ -358,17 +358,25 @@
     b_chain = gather_ring(NY, y, lambda k, h: seen_b.at[k, pl.ds(h * hz, hz)], at_y)
     advance(b_chain, 1)
     advance(a_chain, 1)
+    def partial(k, seen, cols, add):
+        c = dot3([ref[:, :, cols].reshape(2 * block_rows, -1) for ref in (s_high, s_low)],
+                 split(seen[(y + k) % NY].reshape(per, seen.shape[3])), NT)
+        c = c.reshape(NX, 2, own, per).swapaxes(0, 1)
+        cross[k] = cross[k] + c if add else c
+
+    partial(0, seen_b, slice(wide_a, None), False)
     advance(a_chain, 1)
     advance(a_chain, 1)
     advance(b_chain, 1)
+    partial(1, seen_b, slice(wide_a, None), False)
+    partial(3, seen_b, slice(wide_a, None), False)
     drain(a_chain)
 
     def covariance(k):
         there_y = (y + k) % NY
-        o = [seen[there_y].reshape(per, seen.shape[3]) for seen in (seen_a, seen_b)]
-        c = dot3([ref[...].reshape(2 * block_rows, half_members) for ref in (s_high, s_low)],
-                 split(jnp.concatenate(o, axis=1)), NT)
-        cross[k] = c.reshape(NX, 2, own, per).swapaxes(0, 1)
+        if k == NY // 2:
+            partial(k, seen_b, slice(wide_a, None), False)
+        partial(k, seen_a, slice(0, wide_a), True)
         pair = put(cross.at[k, 1 - core], cross_in.at[k], at_x(x, 1 - core))
         yield
         pair.wait_recv()

time: 109 us -> 109 us (level)
  no operation moved by 1% of the time
where the time goes in v4:
time: 109 us; the launch traced here: 108 us
  Pallas kernels  106 us (97%)
  local copies, waits for them, and re-layouts  2.46 us (2%)
    pallas_call x1, Pallas kernels, on_device(): pl.pallas_call(kernel, out_shape=jax.ShapeDtypeStruct((block_rows, member...  106 us
    unnamed x1, local copies, waits for them, and re-layouts  2.46 us

profile of v4, /device:TPU:1, one launch (start us, length us, event | category | flops | bytes accessed | tf_op | source)
XLA Modules:
  0.0 108.5 jit_solution(16410499746403576933)
XLA Ops:
  0.0 106.0 %shard_map.64 = f32[256,1280]{1,0:T(8,128)} custom-call(f32[256,1280]{1,0:T(8,128)} %state_far.1, s32[1280]{0:T(1024)} %level_far.1, f32[4]{0:T(128)} %level_weight.1, s32[1024]{0:T(1024)} %obs_far.1, s32[2,16384]{1,0:T(2,128)} %coords_far.1, f32[16,1280]{1,0:T(8,128)} %w_far.1), custom_call_target="tpu_custom_call" | custom-call | tf_op jit(solution)/shard_map/pallas_call | solution.py:450
  106.0 2.5 %copy.8 = f32[256,1280]{1,0:T(8,128)} copy(f32[256,1280]{1,0:T(8,128)} %shard_map.64) | data formatting | bytes 2621440
